TPU v7x, 128 devices: a whole 4x4x4 slice. The times are simulated.
128 devices in a mesh: blk: 64 (over z, y, x_hi, core), head: 2 (over x_lo).
Axes of the slice: x: 4 (x_hi: 2, x_lo: 2; x = x_hi * 2 + x_lo), y: 4, z: 4, core: 2. Of those that a mesh axis runs over, the one named last changes fastest.
Arguments:
- queries: bfloat16 [16384, 1024], P('blk', 'head'), may hold values from -216 to 216
- keys: bfloat16 [16384, 1024], P('blk', 'head'), may hold values from -6 to 6
- values: bfloat16 [16384, 1024], P('blk', 'head'), may hold values from -6 to 6
- group_table: int32 [64, 2], P('blk'), may hold values from 0 to 127, as said below
- doc_ids: int32 [16384], replicated, may hold values from 0 to 15, never falling along the last dimension, each value on 1 to 8192 neighbouring positions
Outputs:
- attended: bfloat16 [16384, 1024], P('blk', 'head')
Inputs may be any that keep to these rules, and one draw needn't show every extreme that they name: group_table[d, 1] = 127 - group_table[d, 0]; the first column holds each of 0 to 63 once. `doc_ids`: document numbers never fall along positions; a document holds at most 8192 positions.
All inputs are finite; a program needn't handle non-finite values.
Results may differ from a plain program's by a relative error of at most 0.0049.
Values may be sent and summed in bfloat16 or wider, within the bound.
A program may use at most 192 MiB of HBM per device.

v0:
```python
import math

import jax
import jax.numpy as jnp
from jax import lax
from jax.sharding import Mesh
from jax.sharding import PartitionSpec as P

HEAD_DIM = 128
BLK = ("blk_0", "blk_1", "blk_2", "blk_3")


def laid_out(tiles, dim):
    tiles = jnp.moveaxis(tiles, 0, dim)
    lengths = tiles.shape
    return tiles.reshape(*lengths[:dim], lengths[dim] * lengths[dim + 1], *lengths[dim + 2 :])


def stacked_from(x, axes, order):
    tiles = x
    for k in order:
        tiles = lax.all_gather(tiles, axes[k])
    done = order[::-1]
    back = [done.index(k) for k in range(len(axes))]
    tiles = tiles.transpose(*back, *range(len(axes), tiles.ndim))
    return tiles.reshape(-1, *x.shape)


def gather_axes(x, axes, order, dim):
    return laid_out(stacked_from(x, axes, order), dim)


def in_one_piece(arrays, axis, dim, along):
    both = jnp.concatenate(arrays, axis=along)
    out, at, done = (lax.all_gather(both, axis, axis=dim, tiled=True), 0, [])
    for a in arrays:
        done.append(lax.slice_in_dim(out, at, at + a.shape[along], axis=along))
        at += a.shape[along]
    return tuple(done)


def shards(queries, keys, values, group_table, doc_ids):
    tok_rows = queries.shape[0]
    group_rows = tok_rows // 2
    head_count = queries.shape[1] // HEAD_DIM
    score_scale = 1.0 / math.sqrt(HEAD_DIM)
    whole_table = gather_axes(group_table, (("blk_0", "blk_1", "blk_2"), "blk_3"), (0, 1), 0)
    group_docs = doc_ids.reshape(doc_ids.shape[0] // group_rows, group_rows)
    within = jnp.arange(group_rows, dtype=jnp.int32)
    stored_groups = whole_table.reshape(-1)
    all_key_pos = (stored_groups[:, None] * group_rows + within[None, :]).reshape(-1)
    all_key_doc = group_docs[stored_groups].reshape(-1)
    local_groups = group_table.reshape(-1)
    query_pos = (local_groups[:, None] * group_rows + within[None, :]).reshape(-1)
    query_doc = group_docs[local_groups].reshape(-1)
    query_heads = queries.reshape(tok_rows, head_count, HEAD_DIM)

    def attend_shard(running_state, key_piece, value_piece, offset):
        piece_rows = key_piece.shape[0]
        key_pos = lax.dynamic_slice_in_dim(all_key_pos, offset, piece_rows, 0)
        key_doc = lax.dynamic_slice_in_dim(all_key_doc, offset, piece_rows, 0)
        visible = (query_doc[:, None] == key_doc[None, :]) & (
            key_pos[None, :] <= query_pos[:, None]
        )
        summed, running_max, weight_sum = running_state
        key_heads = key_piece.reshape(piece_rows, head_count, HEAD_DIM)
        value_heads = value_piece.reshape(piece_rows, head_count, HEAD_DIM)
        scores = (
            jnp.einsum("qhd,khd->hqk", query_heads, key_heads, preferred_element_type=jnp.float32)
            * score_scale
        )
        scores = jnp.where(visible[None], scores, -1e30)
        new_max = jnp.maximum(running_max, jnp.max(scores, axis=-1))
        weights = jnp.where(visible[None], jnp.exp(scores - new_max[..., None]), 0.0)
        factor = jnp.exp(running_max - new_max)
        weight_sum = weight_sum * factor + jnp.sum(weights, axis=-1)
        summed = summed * jnp.transpose(factor)[..., None] + jnp.einsum(
            "hqk,khd->qhd",
            weights.astype(jnp.bfloat16),
            value_heads,
            preferred_element_type=jnp.float32,
        )
        return (summed, new_max, weight_sum)

    initial = (
        jnp.zeros((tok_rows, head_count, HEAD_DIM), jnp.float32),
        jnp.full((head_count, tok_rows), -1e30, jnp.float32),
        jnp.zeros((head_count, tok_rows), jnp.float32),
    )
    key_piece, value_piece = in_one_piece((keys, values), BLK, 0, 1)
    shard_count = key_piece.shape[0] // tok_rows
    key_shards = key_piece.reshape(shard_count, tok_rows, key_piece.shape[1])
    value_shards = value_piece.reshape(shard_count, tok_rows, value_piece.shape[1])
    shard_ids = jnp.arange(shard_count, dtype=jnp.int32)

    def step(state_now, item):
        key_one, value_one, shard_index = item
        start = shard_index * tok_rows
        return (attend_shard(state_now, key_one, value_one, start), None)

    final_state, unused = lax.scan(step, initial, (key_shards, value_shards, shard_ids))
    summed, running_max, weight_sum = final_state
    output = summed / jnp.transpose(weight_sum)[..., None]
    return output.reshape(tok_rows, head_count * HEAD_DIM).astype(jnp.bfloat16)


def solution(mesh):
    split = Mesh(
        mesh.devices.reshape(4, 4, 2, 2, mesh.shape["head"]),
        ("blk_0", "blk_1", "blk_2", "blk_3", "head"),
    )
    return jax.shard_map(
        shards,
        mesh=split,
        in_specs=(P(BLK, "head"), P(BLK, "head"), P(BLK, "head"), P(BLK, None), P()),
        out_specs=P(BLK, "head"),
        check_vma=False,
    )
```

profile of v0, /device:TPU:8, one launch (start us, length us, event | category | flops | bytes accessed | tf_op | source)
XLA Modules:
  0.0 456.2 jit_solution(2420685313489337652)
XLA Ops:
  6.5 1.9 pad_maximum_fusion
  8.5 93.0 %all-gather.2 = s32[32,1,2]{2,1,0:T(1,128)S(1)} all-gather(s32[1,1,2]{2,1,0:T(1,128)} %bitcast.79), channel_id=2, replica_groups=mesh['blk_0'=4,'blk_1'=4,'blk_2'=2,'blk_3'=2,'head'=2] {'blk_0','blk_1',..., dimensions={0}, use_global_device_ids=true | all-gather | bytes 264 | tf_op jit(solution)/shard_map/all_gather | solution.py:22
  101.6 1.8 all-gather.3
  105.8 1.1 copy.26
  107.8 61.1 %all-gather.6.cloned.1.call-done = bf16[16384,1024]{1,0:T(8,128)(2,1)} async-done(((bf16[256,1024]{1,0:T(8,128)(2,1)}), bf16[16384,1024]{1,0:T(8,128)(2,1)}) %all-gather.6.cloned.1.call-update) | async-done | bytes 33554448 | tf_op jit(solution)/shard_map/all_gather | solution.py:35
  168.9 22.5 %fusion.17 = (bf16[16384,512]{1,0:T(8,128)(2,1)}, bf16[16384,512]{1,0:T(8,128)(2,1)}) fusion(bf16[16384,1024]{1,0:T(8,128)(2,1)} %all-gather.6.cloned.1.call-done), kind=kLoop, calls=%fused_computation.37 | loop fusion | bytes 67108864 | tf_op jit(solution)/shard_map/slice | solution.py:37
  191.4 257.1 %while.15 = (s32[]{:T(128)}, f32[256,4,128]{0,2,1:T(8,128)S(1)}, f32[4,256]{1,0:T(4,128)S(1)}, f32[4,256]{1,0:T(4,128)S(1)}, s32[2,128]{1,0:T(2,128)S(1)}, /*ind...) while((s32[]{:T(128)}, f32[256,4,128]{0,2,1:T(8,128)S(1)}, ...), condition=%wide.region_3.4_spmd.clone, body=%wide.region_0.3_spmd.clone.sunk | while | flops 137173248 | bytes 7415023 | solution.py:101
  197.0 1.1 constant_dynamic-slice_fusion.3
  201.0 1.1 constant_dynamic-slice_fusion.3
  217.1 1.1 constant_dynamic-slice_fusion.3
  221.1 1.1 constant_dynamic-slice_fusion.3
  225.1 1.1 constant_dynamic-slice_fusion.3
  229.2 1.1 constant_dynamic-slice_fusion.3
  233.2 1.1 constant_dynamic-slice_fusion.3
  237.2 1.1 constant_dynamic-slice_fusion.3
  257.3 1.1 constant_dynamic-slice_fusion.3
  261.3 1.1 constant_dynamic-slice_fusion.3
  265.3 1.1 constant_dynamic-slice_fusion.3
  269.3 1.1 constant_dynamic-slice_fusion.3
  273.3 1.1 constant_dynamic-slice_fusion.3
  277.4 1.1 constant_dynamic-slice_fusion.3
  289.4 1.1 constant_dynamic-slice_fusion.3
  293.4 1.1 constant_dynamic-slice_fusion.3
  297.4 1.1 constant_dynamic-slice_fusion.3
  301.5 1.1 constant_dynamic-slice_fusion.3
  305.5 1.1 constant_dynamic-slice_fusion.3
  309.5 1.1 constant_dynamic-slice_fusion.3
  329.6 1.1 constant_dynamic-slice_fusion.3
  333.6 1.1 constant_dynamic-slice_fusion.3
  337.6 1.1 constant_dynamic-slice_fusion.3
  341.6 1.1 constant_dynamic-slice_fusion.3
  345.6 1.1 constant_dynamic-slice_fusion.3
  (898 shorter events, 189.5 us)
Async XLA Ops:
  6.5 97.4 %copy-start = (s32[16384]{0:T(1024)S(1)}, s32[16384]{0:T(1024)}, u32[]{:S(2)}) copy-start(s32[16384]{0:T(1024)} %param.11) | copy-start | bytes 196612
  6.5 162.4 %all-gather.6.cloned.1.call-start = ((), (), s32[]{:S(2)}) async-start(), calls=%async_computation | async-start | bytes 34078720 | tf_op jit(solution)/shard_map/all_gather | solution.py:35
  191.4 258.0 %copy-start.1 = (s32[16384]{0:T(1024)S(1)}, s32[16384]{0:T(1024)}, u32[]{:S(2)}) copy-start(s32[16384]{0:T(1024)} %param.11) | copy-start | bytes 196612
Sparse Core Ops, SparseCore 0:
  10.4 158.4 all-gather.5
where the time goes:
time: 461 us; the launch traced here: 456 us
  local copies, waits for them, and re-layouts  160 us (35%)
  blocking collectives  94.8 us (21%)
  waiting for transfers between devices  61.1 us (13%)
  matrix products  50 us (11%)
  loops' own time  45.1 us (10%)
  other arithmetic  31.8 us (7%)
  between operations  13.5 us (3%)
    dynamic_slice x256, local copies, waits for them, and re-layouts, shards(): lax.scan(step, initial, (key_shards, value_shards, shard_ids))  124 us
    all_gather x2, blocking collectives, stacked_from(): tiles = lax.all_gather(tiles, axes[k])  94.8 us
    all_gather x1, waiting for transfers between devices, in_one_piece(): out, at, done = (lax.all_gather(both, axis, axis=dim, tiled=True), 0, [])  61.1 us
    another operation x1, loops' own time, shards(): lax.scan(step, initial, (key_shards, value_shards, shard_ids))  45.1 us
    dot_general x64, matrix products, attend_shard(): jnp.einsum('hqk,khd->qhd', weights.astype(jnp.bfloat16), value_heads, pre...  26.3 us
    dot_general x64, matrix products, attend_shard(): jnp.einsum('qhd,khd->hqk', query_heads, key_heads, preferred_element_type...  23.7 us
    slice x1, local copies, waits for them, and re-layouts, in_one_piece(): done.append(lax.slice_in_dim(out, at, at + a.shape[along], axis=along))  22.5 us
    reduce_sum x64, other arithmetic, attend_shard(): weight_sum = weight_sum * factor + jnp.sum(weights, axis=-1)  13.3 us
  transfers between devices with their start and end apart: 1, of which 1 were waited for; matrix products, arithmetic and copies ran while one was open for 1% of the time, Pallas kernels for 0%

commit v1 on v0

v1 whole, which is shorter than its diff:
```python
import math

import jax
import jax.numpy as jnp
from jax import lax
from jax.experimental import pallas as pl
from jax.experimental.pallas import tpu as pltpu
from jax.sharding import Mesh
from jax.sharding import PartitionSpec as P

HEAD_DIM = 128
GROUP = 128
GROUPS = 128
AXES = ("z", "y", "xh", "core", "head")
BLK = AXES[:4]
MESH = pl.DeviceIdType.MESH
PART = 2 * GROUP + 16
NEG = -1e30
MASKED = -3e38
FAR = 1 << 20
TILE = 4
COEF = math.log2(math.e) / math.sqrt(HEAD_DIM)


def place():
    return tuple(lax.axis_index(a) for a in AXES)


def remote(src, dst, send, recv, to):
    return pltpu.make_async_remote_copy(
        src_ref=src, dst_ref=dst, send_sem=send, recv_sem=recv, device_id=to, device_id_type=MESH
    )


def spread_kernel(q_ref, k_ref, v_ref, table_ref, doc_ref, kv_out, q_out, start_out, src, loc, snd, own, yp, ym, rp, rm, dd, qr):
    z, y, xh, c, hd = place()
    up, down = lax.rem(y + 1, 4), lax.rem(y + 3, 4)
    zs = [z, lax.rem(z + 1, 4), lax.rem(z + 2, 4), lax.rem(z + 3, 4)]
    to_up, to_down, to_core = (z, up, xh, c, hd), (z, down, xh, c, hd), (z, y, xh, 1 - c, hd)
    partners = [(zs[dz], y, xh, c, hd) for dz in (1, 2, 3)]
    partners += [(zs[dz], y, 1 - xh, c, hd) for dz in range(4)] + [to_up, to_down, to_core]
    barrier = pltpu.get_barrier_semaphore()
    for to in partners:
        pl.semaphore_signal(barrier, inc=1, device_id=to, device_id_type=MESH)

    first = table_ref[0, 0].astype(jnp.float32)
    for h in range(4):
        cols = slice(h * HEAD_DIM, (h + 1) * HEAD_DIM)
        for s in range(2):
            rows = slice(s * GROUP, (s + 1) * GROUP)
            src[h, 0, rows, :] = k_ref[rows, cols]
            src[h, 1, rows, :] = v_ref[rows, cols].T
            src[h, 2, rows, :] = q_ref[rows, cols].T
        for p in range(3):
            src[h, p, 2 * GROUP :, :] = jnp.full((16, HEAD_DIM), first, jnp.float32).astype(jnp.bfloat16)
    docs = doc_ref[...]
    for d in range(16):
        counted = jnp.sum(jnp.where(docs < d, 1, 0), axis=0, keepdims=True)
        start_out[d : d + 1, :] = jnp.broadcast_to(jnp.sum(counted, axis=1, keepdims=True), (1, 128))
    pl.semaphore_wait(barrier, len(partners))

    sent = []

    def start(src_ref, dst_ref, recv, to):
        copy = remote(src_ref, dst_ref, snd.at[len(sent)], recv, to)
        copy.start()
        sent.append(copy)

    def landed(dst_ref, recv):
        remote(dst_ref, dst_ref, snd.at[0], recv, to_core).wait_recv()

    def chunk(zz, yy, cc):
        return kv_out.at[(zz * 4 + yy) * 2 + cc]

    order = (0, 1, 3, 2)
    for dz in order[1:]:
        start(src.at[zs[dz], pl.ds(0, 2)], chunk(z, y, c), own.at[dz], (zs[dz], y, xh, c, hd))
    keep = pltpu.make_async_copy(src.at[z, pl.ds(0, 2)], chunk(z, y, c), loc.at[0])
    keep.start()
    came = [zs[(4 - dz) % 4] for dz in order]

    def first_hop(s):
        mine = chunk(came[s], y, c)
        here = src.at[z, pl.ds(0, 2)]
        if s > 0:
            landed(mine, own.at[order[s]])
            here = mine
        start(here, mine, yp.at[s], to_up)
        start(here, mine, ym.at[s], to_down)
        start(here, mine, dd.at[s, 0], to_core)

    def second_hop(s):
        below, above = chunk(came[s], down, c), chunk(came[s], up, c)
        landed(below, yp.at[s])
        start(below.at[0], below.at[0], rp.at[s], to_up)
        start(below, below, dd.at[s, 1], to_core)
        landed(above, ym.at[s])
        start(above.at[1], above.at[1], rm.at[s], to_down)
        start(above, above, dd.at[s, 2], to_core)

    def last_hop(s):
        across = chunk(came[s], lax.rem(y + 2, 4), c)
        landed(across.at[0], rp.at[s])
        start(across.at[0], across.at[0], dd.at[s, 3], to_core)
        landed(across.at[1], rm.at[s])
        start(across.at[1], across.at[1], dd.at[s, 4], to_core)

    first_hop(0)
    q_mine = q_out.at[z * 2 + xh]
    keep_q = pltpu.make_async_copy(src.at[z, 2], q_mine, loc.at[1])
    keep_q.start()
    for dz in (1, 3, 2, 0):
        for dx in (1, 0):
            if dz or dx:
                to = (zs[dz], y, 1 - xh if dx else xh, c, hd)
                start(src.at[zs[dz], 2], q_mine, qr.at[dz * 2 + dx], to)
    first_hop(1)
    second_hop(0)
    first_hop(2)
    second_hop(1)
    last_hop(0)
    first_hop(3)
    second_hop(2)
    last_hop(1)
    second_hop(3)
    last_hop(2)
    last_hop(3)

    for dz in range(4):
        for dx in range(2):
            if dz or dx:
                landed(q_out.at[zs[(4 - dz) % 4] * 2 + (1 - xh if dx else xh)], qr.at[dz * 2 + dx])
    for s in range(4):
        other = [chunk(came[s], yy, 1 - c) for yy in (y, down, up, lax.rem(y + 2, 4))]
        for i in range(3):
            landed(other[i], dd.at[s, i])
        landed(other[3].at[0], dd.at[s, 3])
        landed(other[3].at[1], dd.at[s, 4])
    keep.wait()
    keep_q.wait()
    for copy in sent:
        copy.wait_send()


def attend_kernel(kv_hbm, q_hbm, start_hbm, o_ref, l_ref, kv, q, hdr_k, hdr_q, tabv, tabs, starts, inv, lst, pre, sems):
    small = [
        pltpu.make_async_copy(kv_hbm.at[:, 0, pl.ds(2 * GROUP, 16), :], hdr_k, sems.at[0]),
        pltpu.make_async_copy(q_hbm.at[:, pl.ds(2 * GROUP, 16), :], hdr_q, sems.at[1]),
        pltpu.make_async_copy(start_hbm, starts, sems.at[2]),
    ]
    large = [pltpu.make_async_copy(q_hbm, q, sems.at[3])]
    for i in range(4):
        large.append(pltpu.make_async_copy(kv_hbm.at[pl.ds(8 * i, 8)], kv.at[pl.ds(8 * i, 8)], sems.at[4 + i]))
    for copy in small + large:
        copy.start()
    for copy in small:
        copy.wait()
    tabv[0:32, :] = hdr_k[:, 0, :].astype(jnp.float32).astype(jnp.int32)
    tabv[32:40, :] = hdr_q[:, 0, :].astype(jnp.float32).astype(jnp.int32)
    table_copy = pltpu.make_async_copy(tabv, tabs, sems.at[8])
    table_copy.start()

    @pl.loop(0, GROUPS)
    def _(p):
        inv[p] = -1

    table_copy.wait()

    @pl.loop(0, 32)
    def _(i):
        g0 = tabs[i, 0]
        inv[g0] = 2 * i
        inv[GROUPS - 1 - g0] = 2 * i + 1

    def count(p, n):
        pre[p] = n
        lst[n] = inv[p] * GROUPS + p
        return n + jnp.where(inv[p] >= 0, 1, 0)

    pre[GROUPS] = lax.fori_loop(0, GROUPS, count, jnp.int32(0))
    for copy in large:
        copy.wait()

    lane = lax.broadcasted_iota(jnp.int32, (1, GROUP), 1)
    row = lax.broadcasted_iota(jnp.int32, (GROUP, GROUP), 0)

    @pl.loop(0, 16)
    def _(u):
        ch, s = lax.div(u, 2), lax.rem(u, 2)
        g0 = tabs[32 + ch, 0]
        g = jnp.where(s == 0, g0, GROUPS - 1 - g0)
        at = pl.ds(pl.multiple_of(s * GROUP, GROUP), GROUP)
        q_t = q[ch, at, :]
        qpos = g * GROUP + lane
        low, low_first = jnp.zeros_like(lane), jnp.int32(0)
        for d in range(1, 16):
            begin = starts[d, 0]
            low = jnp.where(begin <= qpos, begin, low)
            low_first = jnp.where(begin <= g * GROUP, begin, low_first)
        begin_at, end_at = pre[lax.div(low_first, GROUP)], pre[g + 1]

        def step(t, state):
            top, weight, acc = state
            scores, held = [], []
            for i in range(TILE):
                e = begin_at + t * TILE + i
                entry = lst[jnp.minimum(e, end_at - 1)]
                slot, key_group = lax.div(entry, GROUPS), lax.rem(entry, GROUPS)
                base = jnp.where(e < end_at, key_group * GROUP, FAR)
                where = pl.ds(pl.multiple_of(lax.rem(slot, 2) * GROUP, GROUP), GROUP)
                one = jnp.dot(kv[lax.div(slot, 2), 0, where, :], q_t, preferred_element_type=jnp.float32)
                seen = (row >= low - base) & (row <= qpos - base)
                scores.append(jnp.where(seen, one, MASKED))
                held.append(kv[lax.div(slot, 2), 1, where, :])
            new_top = top
            for one in scores:
                new_top = jnp.maximum(new_top, jnp.max(one, axis=0, keepdims=True))
            factor = jnp.exp2((top - new_top) * COEF)
            weight, acc = weight * factor, acc * factor
            for one, v_t in zip(scores, held):
                part = jnp.exp2((one - new_top) * COEF)
                weight = weight + jnp.sum(part, axis=0, keepdims=True)
                acc = acc + jnp.dot(v_t, part.astype(jnp.bfloat16), preferred_element_type=jnp.float32)
            return new_top, weight, acc

        top, weight, acc = lax.fori_loop(
            0,
            lax.div(end_at - begin_at + TILE - 1, TILE),
            step,
            (
                jnp.full((1, GROUP), NEG, jnp.float32),
                jnp.zeros((1, GROUP), jnp.float32),
                jnp.zeros((HEAD_DIM, GROUP), jnp.float32),
            ),
        )
        some = weight > 0.0
        safe = jnp.where(some, weight, 1.0)
        o_ref[ch, at, :] = (acc / safe).astype(jnp.bfloat16)
        l_ref[ch, pl.ds(s, 1), :] = jnp.where(some, top * COEF + jnp.log2(safe), NEG)


def merge_kernel(o_hbm, l_hbm, out_ref, o_in, l_in, loc, snd, orecv, lrecv):
    z, y, xh, c, hd = place()
    zs = [z, lax.rem(z + 1, 4), lax.rem(z + 2, 4), lax.rem(z + 3, 4)]
    peers = [(dz, dx) for dz in (2, 1, 3, 0) for dx in (1, 0) if dz or dx]
    barrier = pltpu.get_barrier_semaphore()
    for dz, dx in peers:
        to = (zs[dz], y, 1 - xh if dx else xh, c, hd)
        pl.semaphore_signal(barrier, inc=1, device_id=to, device_id_type=MESH)
    mine = z * 2 + xh
    keep = [
        pltpu.make_async_copy(o_hbm.at[mine], o_in.at[mine], loc.at[0]),
        pltpu.make_async_copy(l_hbm.at[mine], l_in.at[mine], loc.at[1]),
    ]
    for copy in keep:
        copy.start()
    pl.semaphore_wait(barrier, len(peers))
    sent = []
    for n, (dz, dx) in enumerate(peers):
        side = 1 - xh if dx else xh
        to, theirs = (zs[dz], y, side, c, hd), zs[dz] * 2 + side
        for src, dst, recv in ((o_hbm, o_in, orecv), (l_hbm, l_in, lrecv)):
            copy = remote(src.at[theirs], dst.at[mine], snd.at[len(sent)], recv.at[dz * 2 + dx], to)
            copy.start()
            sent.append(copy)
    for copy in keep:
        copy.wait()
    for dz, dx in peers:
        side = 1 - xh if dx else xh
        theirs = zs[(4 - dz) % 4] * 2 + side
        to = (zs[1], y, xh, c, hd)
        remote(o_hbm.at[0], o_in.at[theirs], snd.at[0], orecv.at[dz * 2 + dx], to).wait_recv()
        remote(l_hbm.at[0], l_in.at[theirs], snd.at[0], lrecv.at[dz * 2 + dx], to).wait_recv()
    for h in range(4):
        for s in range(2):
            rows = slice(s * GROUP, (s + 1) * GROUP)
            a, b = l_in[2 * h, s : s + 1, :], l_in[2 * h + 1, s : s + 1, :]
            most = jnp.maximum(a, b)
            wa, wb = jnp.exp2(a - most), jnp.exp2(b - most)
            total = wa + wb
            merged = o_in[2 * h, rows, :].astype(jnp.float32) * (wa / total)
            merged = merged + o_in[2 * h + 1, rows, :].astype(jnp.float32) * (wb / total)
            out_ref[rows, h * HEAD_DIM : (h + 1) * HEAD_DIM] = merged.T.astype(jnp.bfloat16)
    for copy in sent:
        copy.wait_send()


def shards(queries, keys, values, group_table, doc_ids):
    vmem = pl.BlockSpec(memory_space=pltpu.VMEM)
    hbm = pl.BlockSpec(memory_space=pl.ANY)
    smem = pl.BlockSpec(memory_space=pltpu.SMEM)
    dma = pltpu.SemaphoreType.DMA
    kv, q, begins = pl.pallas_call(
        spread_kernel,
        out_shape=(
            jax.ShapeDtypeStruct((32, 2, PART, HEAD_DIM), jnp.bfloat16),
            jax.ShapeDtypeStruct((8, PART, HEAD_DIM), jnp.bfloat16),
            jax.ShapeDtypeStruct((16, 128), jnp.int32),
        ),
        in_specs=[vmem, vmem, vmem, smem, vmem],
        out_specs=(hbm, hbm, vmem),
        scratch_shapes=[
            pltpu.VMEM((4, 3, PART, HEAD_DIM), jnp.bfloat16),
            dma((2,)), dma((46,)), dma((4,)), dma((4,)), dma((4,)), dma((4,)), dma((4,)), dma((4, 5)), dma((8,)),
        ],
        compiler_params=pltpu.CompilerParams(collective_id=0, has_side_effects=True),
    )(queries, keys, values, group_table, doc_ids.reshape(128, 128))
    o, l = pl.pallas_call(
        attend_kernel,
        out_shape=(
            jax.ShapeDtypeStruct((8, 2 * GROUP, HEAD_DIM), jnp.bfloat16),
            jax.ShapeDtypeStruct((8, 8, GROUP), jnp.float32),
        ),
        in_specs=[hbm, hbm, hbm],
        out_specs=(vmem, vmem),
        scratch_shapes=[
            pltpu.VMEM((32, 2, PART, HEAD_DIM), jnp.bfloat16),
            pltpu.VMEM((8, PART, HEAD_DIM), jnp.bfloat16),
            pltpu.VMEM((32, 16, HEAD_DIM), jnp.bfloat16),
            pltpu.VMEM((8, 16, HEAD_DIM), jnp.bfloat16),
            pltpu.VMEM((40, 128), jnp.int32),
            pltpu.SMEM((40, 128), jnp.int32),
            pltpu.SMEM((16, 128), jnp.int32),
            pltpu.SMEM((GROUPS,), jnp.int32),
            pltpu.SMEM((GROUPS,), jnp.int32),
            pltpu.SMEM((GROUPS + 8,), jnp.int32),
            dma((9,)),
        ],
    )(kv, q, begins)
    return pl.pallas_call(
        merge_kernel,
        out_shape=jax.ShapeDtypeStruct(queries.shape, jnp.bfloat16),
        in_specs=[hbm, hbm],
        out_specs=vmem,
        scratch_shapes=[
            pltpu.VMEM((8, 2 * GROUP, HEAD_DIM), jnp.bfloat16),
            pltpu.VMEM((8, 8, GROUP), jnp.float32),
            dma((2,)), dma((14,)), dma((8,)), dma((8,)),
        ],
        compiler_params=pltpu.CompilerParams(collective_id=1, has_side_effects=True),
    )(o, l)


def solution(mesh):
    split = Mesh(mesh.devices.reshape(4, 4, 2, 2, mesh.shape["head"]), AXES)
    return jax.shard_map(
        shards,
        mesh=split,
        in_specs=(P(BLK, "head"), P(BLK, "head"), P(BLK, "head"), P(BLK, None), P()),
        out_specs=P(BLK, "head"),
        check_vma=False,
    )
```

time: 461 us -> 82.1 us (0.18)
  local copies, waits for them, and re-layouts: 160 us -> 1.67 us
  blocking collectives: 94.8 us -> 0 us
  Pallas kernels: 0 us -> 80.2 us
  waiting for transfers between devices: 61.1 us -> 0 us
  matrix products: 50 us -> 0 us
  loops' own time: 45.1 us -> 0 us
  other arithmetic: 31.8 us -> 0 us
  between operations: 13.5 us -> 0.02 us
    dynamic_slice x384 -> x0, local copies, waits for them, and re-layouts: 133 us -> none  [the longest x256 124 us: shards(): lax.scan(step, initial, (key_shards, value_shards, shard_ids))]
    all_gather x2 -> x0, blocking collectives: 94.8 us -> none  [stacked_from(): tiles = lax.all_gather(tiles, axes[k])]
    pallas_call x0 -> x3, Pallas kernels: none -> 80.2 us  [the longest x1 37 us: shards(): pl.pallas_call(spread_kernel, out_shape=(jax.ShapeDtypeStruct((32, 2, PAR...]
    all_gather x1 -> x0, waiting for transfers between devices: 61.1 us -> none  [in_one_piece(): out, at, done = (lax.all_gather(both, axis, axis=dim, tiled=True), 0, [])]
    dot_general x128 -> x0, matrix products: 50 us -> none  [the longest x64 26.3 us: attend_shard(): jnp.einsum('hqk,khd->qhd', weights.astype(jnp.bfloat16), value_heads, pre...]
    another operation x1 -> x0, loops' own time: 45.1 us -> none  [shards(): lax.scan(step, initial, (key_shards, value_shards, shard_ids))]
    slice x1 -> x0, local copies, waits for them, and re-layouts: 22.5 us -> none  [in_one_piece(): done.append(lax.slice_in_dim(out, at, at + a.shape[along], axis=along))]
    reduce_sum x64 -> x0, other arithmetic: 13.3 us -> none  [attend_shard(): weight_sum = weight_sum * factor + jnp.sum(weights, axis=-1)]
  transfers between devices with their start and end apart: 1 -> 0, of which waited for: 1 -> 0; matrix products, arithmetic and copies ran while one was open for 1% -> 0% of each run, Pallas kernels for 0% -> 0%
where the time goes in v1:
time: 82.1 us; the launch traced here: 81.9 us
  Pallas kernels  80.2 us (98%)
  local copies, waits for them, and re-layouts  1.67 us (2%)
    pallas_call x1, Pallas kernels, shards(): pl.pallas_call(spread_kernel, out_shape=(jax.ShapeDtypeStruct((32, 2, PAR...  37 us
    pallas_call x1, Pallas kernels, shards(): pl.pallas_call(attend_kernel, out_shape=(jax.ShapeDtypeStruct((8, 2 * GRO...  27.1 us
    pallas_call x1, Pallas kernels, shards(): pl.pallas_call(merge_kernel, out_shape=jax.ShapeDtypeStruct(queries.shape...  16.1 us
    unnamed x1, local copies, waits for them, and re-layouts  1.67 us

profile of v1, /device:TPU:8, one launch (start us, length us, event | category | flops | bytes accessed | tf_op | source)
XLA Modules:
  0.0 81.9 jit_solution(16108019066469245181)
XLA Ops:
  0.0 37.0 %shard_map.55 = (bf16[32,2,272,128]{3,2,1,0:T(8,128)(2,1)}, bf16[8,272,128]{2,1,0:T(8,128)(2,1)}, s32[16,128]{1,0:T(8,128)}) custom-call(bf16[256,512]{1,0:T(8,128)(2,1)} %q_ref.1, bf16[256,512]{1,0:T(8,128)(2,1)} %k_ref.1, bf16[256,512]{1,0:T(8,128)(2,1)} %v_ref.1, s32[1,2]{1,0:T(1,128)} %table_ref.1, s32[128,128]{1,0:T(8,128)} %bitcast.1), custom_call_target="tpu_custom_call" | custom-call | tf_op jit(solution)/shard_map/pallas_call | solution.py:293
  37.0 27.1 %shard_map.56 = (bf16[8,256,128]{2,1,0:T(8,128)(2,1)}, f32[8,8,128]{2,1,0:T(8,128)}) custom-call(bf16[32,2,272,128]{3,2,1,0:T(8,128)(2,1)} %get-tuple-element.10.kv_hbm, bf16[8,272,128]{2,1,0:T(8,128)(2,1)} %get-tuple-element.11.q_hbm, s32[16,128]{1,0:T(8,128)} %get-tuple-element.12.start_hbm), custom_call_target="tpu_custom_call" | custom-call | tf_op jit(solution)/shard_map/pallas_call | solution.py:308
  64.1 16.1 %shard_map.57 = bf16[256,512]{1,0:T(8,128)(2,1)} custom-call(bf16[8,256,128]{2,1,0:T(8,128)(2,1)} %get-tuple-element.13.o_hbm, f32[8,8,128]{2,1,0:T(8,128)} %get-tuple-element.14.l_hbm), custom_call_target="tpu_custom_call" | custom-call | tf_op jit(solution)/shard_map/pallas_call | solution.py:330
  80.2 1.7 %copy.7 = bf16[256,512]{1,0:T(8,128)(2,1)} copy(bf16[256,512]{1,0:T(8,128)(2,1)} %shard_map.57) | data formatting | bytes 524288

commit v2 on v1

v2 whole, which is shorter than its diff:
```python
import math

import jax
import jax.numpy as jnp
from jax import lax
from jax.experimental import pallas as pl
from jax.experimental.pallas import tpu as pltpu
from jax.sharding import Mesh
from jax.sharding import PartitionSpec as P

HEAD_DIM = 128
GROUP = 128
GROUPS = 128
AXES = ("z", "y", "xh", "core", "head")
BLK = AXES[:4]
MESH = pl.DeviceIdType.MESH
PART = 2 * GROUP + 16
NEG = -1e30
MASKED = -3e38
FAR = 1 << 20
TILE = 4
COEF = math.log2(math.e) / math.sqrt(HEAD_DIM)


def place():
    return tuple(lax.axis_index(a) for a in AXES)


def remote(src, dst, send, recv, to):
    return pltpu.make_async_remote_copy(
        src_ref=src, dst_ref=dst, send_sem=send, recv_sem=recv, device_id=to, device_id_type=MESH
    )


def spread_kernel(q_ref, k_ref, v_ref, table_ref, doc_ref, kv_out, q_out, start_out, src, snd, own, yp, ym, rp, rm, dd, qr):
    z, y, xh, c, hd = place()
    up, down = lax.rem(y + 1, 4), lax.rem(y + 3, 4)
    zs = [z, lax.rem(z + 1, 4), lax.rem(z + 2, 4), lax.rem(z + 3, 4)]
    to_up, to_down, to_core = (z, up, xh, c, hd), (z, down, xh, c, hd), (z, y, xh, 1 - c, hd)
    partners = [(zs[dz], y, xh, c, hd) for dz in (1, 2, 3)]
    partners += [(zs[dz], y, 1 - xh, c, hd) for dz in range(4)] + [to_up, to_down, to_core]
    barrier = pltpu.get_barrier_semaphore()
    for to in partners:
        pl.semaphore_signal(barrier, inc=1, device_id=to, device_id_type=MESH)

    first = table_ref[0, 0].astype(jnp.float32)
    for h in range(4):
        cols = slice(h * HEAD_DIM, (h + 1) * HEAD_DIM)
        for s in range(2):
            rows = slice(s * GROUP, (s + 1) * GROUP)
            src[h, 0, rows, :] = k_ref[rows, cols]
            src[h, 1, rows, :] = v_ref[rows, cols].T
            src[h, 2, rows, :] = q_ref[rows, cols].T
        for p in range(3):
            src[h, p, 2 * GROUP :, :] = jnp.full((16, HEAD_DIM), first, jnp.float32).astype(jnp.bfloat16)
    docs = doc_ref[...]
    for d in range(16):
        counted = jnp.sum(jnp.where(docs < d, 1, 0), axis=0, keepdims=True)
        start_out[d : d + 1, :] = jnp.broadcast_to(jnp.sum(counted, axis=1, keepdims=True), (1, 128))
    pl.semaphore_wait(barrier, len(partners))

    sent = []

    def start(src_ref, dst_ref, recv, to):
        copy = remote(src_ref, dst_ref, snd.at[len(sent)], recv, to)
        copy.start()
        sent.append(copy)

    def landed(dst_ref, recv):
        remote(dst_ref, dst_ref, snd.at[0], recv, to_core).wait_recv()

    def chunk(zz, yy, cc):
        return kv_out.at[(zz * 4 + yy) * 2 + cc]

    order = (0, 1, 3, 2)
    for dz in order[1:]:
        start(src.at[zs[dz], pl.ds(0, 2)], chunk(z, y, c), own.at[dz], (zs[dz], y, xh, c, hd))
    kv_out[(z * 4 + y) * 2 + c] = src[z, 0:2]
    came = [zs[(4 - dz) % 4] for dz in order]

    def first_hop(s):
        mine = chunk(came[s], y, c)
        here = src.at[z, pl.ds(0, 2)]
        if s > 0:
            landed(mine, own.at[order[s]])
            here = mine
        start(here, mine, yp.at[s], to_up)
        start(here, mine, ym.at[s], to_down)
        start(here, mine, dd.at[s, 0], to_core)

    def second_hop(s):
        below, above = chunk(came[s], down, c), chunk(came[s], up, c)
        landed(below, yp.at[s])
        start(below.at[0], below.at[0], rp.at[s], to_up)
        start(below, below, dd.at[s, 1], to_core)
        landed(above, ym.at[s])
        start(above.at[1], above.at[1], rm.at[s], to_down)
        start(above, above, dd.at[s, 2], to_core)

    def last_hop(s):
        across = chunk(came[s], lax.rem(y + 2, 4), c)
        landed(across.at[0], rp.at[s])
        start(across.at[0], across.at[0], dd.at[s, 3], to_core)
        landed(across.at[1], rm.at[s])
        start(across.at[1], across.at[1], dd.at[s, 4], to_core)

    first_hop(0)
    q_mine = q_out.at[z * 2 + xh]
    q_out[z * 2 + xh] = src[z, 2]
    for dz in (1, 3, 2, 0):
        for dx in (1, 0):
            if dz or dx:
                to = (zs[dz], y, 1 - xh if dx else xh, c, hd)
                start(src.at[zs[dz], 2], q_mine, qr.at[dz * 2 + dx], to)
    first_hop(1)
    second_hop(0)
    first_hop(2)
    second_hop(1)
    last_hop(0)
    first_hop(3)
    second_hop(2)
    last_hop(1)
    second_hop(3)
    last_hop(2)
    last_hop(3)

    for dz in range(4):
        for dx in range(2):
            if dz or dx:
                landed(q_out.at[zs[(4 - dz) % 4] * 2 + (1 - xh if dx else xh)], qr.at[dz * 2 + dx])
    for s in range(4):
        other = [chunk(came[s], yy, 1 - c) for yy in (y, down, up, lax.rem(y + 2, 4))]
        for i in range(3):
            landed(other[i], dd.at[s, i])
        landed(other[3].at[0], dd.at[s, 3])
        landed(other[3].at[1], dd.at[s, 4])
    for copy in sent:
        copy.wait_send()


def attend_kernel(kv, q, start_ref, o_ref, l_ref, plan, sm, low_s, bias_s, top_s, weight_s, acc_s, s_even, s_odd, sem):
    lane = lax.broadcasted_iota(jnp.int32, (1, 128), 1)
    lane32 = lax.broadcasted_iota(jnp.int32, (32, 128), 1)
    lane16 = lax.broadcasted_iota(jnp.int32, (16, 128), 1)
    code = lax.broadcasted_iota(jnp.int32, (32, 128), 0) * 2
    first = kv[:, 0, 2 * GROUP, :].astype(jnp.float32).astype(jnp.int32)
    second = GROUPS - 1 - first
    at = jnp.where(first == lane32, code + 1, 0) + jnp.where(second == lane32, code + 2, 0)
    inv = jnp.sum(at, axis=0, keepdims=True) - 1
    here = jnp.where(inv >= 0, 1, 0)
    rank0 = jnp.sum(jnp.where(lane32 < first, here, 0), axis=1, keepdims=True)
    rank1 = jnp.sum(jnp.where(lane32 < second, here, 0), axis=1, keepdims=True)
    listed = jnp.where(rank0 == lane32, code * GROUPS, 0) + jnp.where(rank1 == lane32, (code + 1) * GROUPS, 0)
    plan[0:1, :] = jnp.sum(listed, axis=0, keepdims=True)
    plan[1:2, :] = inv

    q_first = q[:, 2 * GROUP, :].astype(jnp.float32).astype(jnp.int32)
    group = jnp.concatenate([q_first, GROUPS - 1 - q_first], axis=0)
    q_pos = group * GROUP + lane16
    low, low_first = jnp.zeros_like(q_pos), jnp.zeros_like(q_pos)
    for d in range(1, 16):
        begin = start_ref[d : d + 1, :]
        low = jnp.where(begin <= q_pos, begin, low)
        low_first = jnp.where(begin <= group * GROUP, begin, low_first)
    low_s[...] = low
    bias_s[...] = jnp.where(low == low_first, 0.0, MASKED)
    low_group = lax.shift_right_logical(low_first, 7)
    plan[16:32, :] = group
    plan[32:48, :] = low_group
    begin_at = jnp.sum(jnp.where(lane16 <= low_group, here, 0), axis=1, keepdims=True)
    end_at = jnp.sum(jnp.where(lane16 < group, here, 0), axis=1, keepdims=True)
    tiles = lax.shift_right_logical(jnp.maximum(end_at - begin_at, 0) + (TILE - 1), 2)
    begin_at, end_at, tiles = (jnp.broadcast_to(x, (16, 128)) for x in (begin_at, end_at, tiles))
    done = jnp.zeros((1, 128), jnp.int32)
    item = [lane, lane + 128, lane + 256]
    item_u, item_at, item_end = [[jnp.zeros((1, 128), jnp.int32) for _ in item] for _ in range(3)]
    for u in range(16):
        after = done + tiles[u : u + 1, :]
        for i, n in enumerate(item):
            mine = (done <= n) & (n < after)
            item_u[i] = jnp.where(mine, u, item_u[i])
            item_at[i] = jnp.where(mine, begin_at[u : u + 1, :] + (n - done) * TILE, item_at[i])
            item_end[i] = jnp.where(mine, end_at[u : u + 1, :], item_end[i])
        done = after
    for i in range(3):
        plan[2 + i : 3 + i, :] = item_u[i]
        plan[5 + i : 6 + i, :] = item_at[i]
        plan[8 + i : 9 + i, :] = item_end[i]
    plan[11:12, :] = done
    copy = pltpu.make_async_copy(plan, sm, sem)
    copy.start()
    copy.wait()

    row = lax.broadcasted_iota(jnp.int32, (GROUP, GROUP), 0)

    def half(slot):
        return pl.ds(pl.multiple_of(lax.rem(slot, 2) * GROUP, GROUP), GROUP)

    def queries_of(u):
        return q[lax.rem(u, 8), pl.ds(pl.multiple_of(lax.div(u, 8) * GROUP, GROUP), GROUP), :]

    @pl.loop(0, 16)
    def _(u):
        g, low_g = sm[16 + u, 0], sm[32 + u, 0]
        q_t = queries_of(u)
        lower = low_s[pl.ds(u, 1), :]
        upper = g * GROUP + lane
        scores, held = [], []
        for key_group, wanted in ((g, True), (low_g, low_g < g)):
            found = sm[1, key_group]
            slot = jnp.maximum(found, 0)
            base = jnp.where((found >= 0) & wanted, key_group * GROUP, FAR)
            one = jnp.dot(kv[lax.div(slot, 2), 0, half(slot), :], q_t, preferred_element_type=jnp.float32)
            seen = (row >= lower - base) & (row <= upper - base)
            scores.append(jnp.where(seen, one, MASKED))
            held.append(kv[lax.div(slot, 2), 1, half(slot), :])
        top = jnp.full((1, GROUP), NEG, jnp.float32)
        for one in scores:
            top = jnp.maximum(top, jnp.max(one, axis=0, keepdims=True))
        parts = [jnp.exp2((one - top) * COEF) for one in scores]
        top_s[pl.ds(u, 1), :] = top
        weight_s[pl.ds(u, 1), :] = sum(jnp.sum(part, axis=0, keepdims=True) for part in parts)
        acc_s[u] = jnp.dot(
            jnp.concatenate(held, axis=1),
            jnp.concatenate([part.astype(jnp.bfloat16) for part in parts], axis=0),
            preferred_element_type=jnp.float32,
        )

    def read(i):
        r, k = lax.shift_right_logical(i, 7), lax.bitwise_and(i, 127)
        return sm[2 + r, k], sm[5 + r, k], sm[8 + r, k]

    def slot_of(e, end):
        return lax.shift_right_logical(sm[0, jnp.maximum(jnp.minimum(e, end - 1), 0)], 7)

    def score(i, dst):
        u, e, end = read(i)
        q_t = queries_of(u)
        for j in range(TILE):
            slot = slot_of(e + j, end)
            dst[j * GROUP : (j + 1) * GROUP, :] = jnp.dot(
                kv[lax.div(slot, 2), 0, half(slot), :], q_t, preferred_element_type=jnp.float32
            )

    def absorb(i, src):
        u, e, end = read(i)
        lanes = bias_s[pl.ds(u, 1), :]
        top = top_s[pl.ds(u, 1), :]
        new_top, biases, held, parts = top, [], [], []
        for j in range(TILE):
            biases.append(jnp.where(e + j < end, lanes, MASKED))
            best = jnp.max(src[j * GROUP : (j + 1) * GROUP, :], axis=0, keepdims=True)
            new_top = jnp.maximum(new_top, best + biases[j])
        factor = jnp.exp2((top - new_top) * COEF)
        weight = weight_s[pl.ds(u, 1), :] * factor
        for j in range(TILE):
            part = jnp.exp2((src[j * GROUP : (j + 1) * GROUP, :] - (new_top - biases[j])) * COEF)
            weight = weight + jnp.sum(part, axis=0, keepdims=True)
            parts.append(part.astype(jnp.bfloat16))
            slot = slot_of(e + j, end)
            held.append(kv[lax.div(slot, 2), 1, half(slot), :])
        top_s[pl.ds(u, 1), :] = new_top
        weight_s[pl.ds(u, 1), :] = weight
        acc_s[u] = acc_s[u] * factor + jnp.dot(
            jnp.concatenate(held, axis=1), jnp.concatenate(parts, axis=0), preferred_element_type=jnp.float32
        )

    total = sm[11, 0]
    score(jnp.int32(0), s_even)

    @pl.loop(0, lax.shift_right_logical(total + 1, 1))
    def _(k):
        i = 2 * k
        score(i + 1, s_odd)
        absorb(i, s_even)
        score(i + 2, s_even)
        absorb(i + 1, s_odd)

    @pl.loop(0, 16)
    def _(u):
        weight = weight_s[pl.ds(u, 1), :]
        some = weight > 0.0
        safe = jnp.where(some, weight, 1.0)
        ch, s = lax.rem(u, 8), lax.div(u, 8)
        o_ref[ch, pl.ds(pl.multiple_of(s * GROUP, GROUP), GROUP), :] = (acc_s[u] * (1.0 / safe)).astype(jnp.bfloat16)
        l_ref[ch, pl.ds(s, 1), :] = jnp.where(some, top_s[pl.ds(u, 1), :] * COEF + jnp.log2(safe), NEG)


def merge_kernel(o_ref, l_ref, out_ref, o_in, l_in, snd, orecv, lrecv):
    z, y, xh, c, hd = place()
    zs = [z, lax.rem(z + 1, 4), lax.rem(z + 2, 4), lax.rem(z + 3, 4)]
    peers = [(dz, dx) for dz in (2, 1, 3, 0) for dx in (1, 0) if dz or dx]
    barrier = pltpu.get_barrier_semaphore()
    for dz, dx in peers:
        to = (zs[dz], y, 1 - xh if dx else xh, c, hd)
        pl.semaphore_signal(barrier, inc=1, device_id=to, device_id_type=MESH)
    mine = z * 2 + xh
    o_in[mine] = o_ref[mine]
    l_in[mine] = l_ref[mine]
    pl.semaphore_wait(barrier, len(peers))
    sent = []
    for n, (dz, dx) in enumerate(peers):
        side = 1 - xh if dx else xh
        to, theirs = (zs[dz], y, side, c, hd), zs[dz] * 2 + side
        for src, dst, recv in ((o_ref, o_in, orecv), (l_ref, l_in, lrecv)):
            copy = remote(src.at[theirs], dst.at[mine], snd.at[len(sent)], recv.at[dz * 2 + dx], to)
            copy.start()
            sent.append(copy)
    for dz, dx in peers:
        side = 1 - xh if dx else xh
        theirs = zs[(4 - dz) % 4] * 2 + side
        to = (zs[1], y, xh, c, hd)
        remote(o_ref.at[0], o_in.at[theirs], snd.at[0], orecv.at[dz * 2 + dx], to).wait_recv()
        remote(l_ref.at[0], l_in.at[theirs], snd.at[0], lrecv.at[dz * 2 + dx], to).wait_recv()
    for h in range(4):
        for s in range(2):
            rows = slice(s * GROUP, (s + 1) * GROUP)
            a, b = l_in[2 * h, s : s + 1, :], l_in[2 * h + 1, s : s + 1, :]
            most = jnp.maximum(a, b)
            wa, wb = jnp.exp2(a - most), jnp.exp2(b - most)
            total = wa + wb
            merged = o_in[2 * h, rows, :].astype(jnp.float32) * (wa / total)
            merged = merged + o_in[2 * h + 1, rows, :].astype(jnp.float32) * (wb / total)
            out_ref[rows, h * HEAD_DIM : (h + 1) * HEAD_DIM] = merged.T.astype(jnp.bfloat16)
    for copy in sent:
        copy.wait_send()


def shards(queries, keys, values, group_table, doc_ids):
    vmem = pl.BlockSpec(memory_space=pltpu.VMEM)
    hbm = pl.BlockSpec(memory_space=pl.ANY)
    smem = pl.BlockSpec(memory_space=pltpu.SMEM)
    dma = pltpu.SemaphoreType.DMA
    kv, q, begins = pl.pallas_call(
        spread_kernel,
        out_shape=(
            pltpu.VMEM((32, 2, PART, HEAD_DIM), jnp.bfloat16),
            pltpu.VMEM((8, PART, HEAD_DIM), jnp.bfloat16),
            pltpu.VMEM((16, 128), jnp.int32),
        ),
        in_specs=[vmem, vmem, vmem, smem, vmem],
        out_specs=(vmem, vmem, vmem),
        scratch_shapes=[
            pltpu.VMEM((4, 3, PART, HEAD_DIM), jnp.bfloat16),
            dma((46,)), dma((4,)), dma((4,)), dma((4,)), dma((4,)), dma((4,)), dma((4, 5)), dma((8,)),
        ],
        compiler_params=pltpu.CompilerParams(collective_id=0, has_side_effects=True, vmem_limit_bytes=16 << 20),
    )(queries, keys, values, group_table, doc_ids.reshape(128, 128))
    o, l = pl.pallas_call(
        attend_kernel,
        out_shape=(
            pltpu.VMEM((8, 2 * GROUP, HEAD_DIM), jnp.bfloat16),
            pltpu.VMEM((8, 8, GROUP), jnp.float32),
        ),
        in_specs=[vmem, vmem, vmem],
        out_specs=(vmem, vmem),
        scratch_shapes=[
            pltpu.VMEM((48, 128), jnp.int32),
            pltpu.SMEM((48, 128), jnp.int32),
            pltpu.VMEM((16, 128), jnp.int32),
            pltpu.VMEM((16, 128), jnp.float32),
            pltpu.VMEM((16, 128), jnp.float32),
            pltpu.VMEM((16, 128), jnp.float32),
            pltpu.VMEM((16, HEAD_DIM, GROUP), jnp.float32),
            pltpu.VMEM((TILE * GROUP, GROUP), jnp.float32),
            pltpu.VMEM((TILE * GROUP, GROUP), jnp.float32),
            dma,
        ],
        compiler_params=pltpu.CompilerParams(vmem_limit_bytes=16 << 20),
    )(kv, q, begins)
    return pl.pallas_call(
        merge_kernel,
        out_shape=jax.ShapeDtypeStruct(queries.shape, jnp.bfloat16),
        in_specs=[vmem, vmem],
        out_specs=vmem,
        scratch_shapes=[
            pltpu.VMEM((8, 2 * GROUP, HEAD_DIM), jnp.bfloat16),
            pltpu.VMEM((8, 8, GROUP), jnp.float32),
            dma((14,)), dma((8,)), dma((8,)),
        ],
        compiler_params=pltpu.CompilerParams(collective_id=1, has_side_effects=True, vmem_limit_bytes=16 << 20),
    )(o, l)


def solution(mesh):
    split = Mesh(mesh.devices.reshape(4, 4, 2, 2, mesh.shape["head"]), AXES)
    return jax.shard_map(
        shards,
        mesh=split,
        in_specs=(P(BLK, "head"), P(BLK, "head"), P(BLK, "head"), P(BLK, None), P()),
        out_specs=P(BLK, "head"),
        check_vma=False,
    )
```

time: 82.1 us -> 71.4 us (0.87)
  Pallas kernels: 80.2 us -> 66 us
  local copies, waits for them, and re-layouts: 1.67 us -> 5.05 us
    pallas_call x2, Pallas kernels: 64.1 us -> 54.3 us  [the longest x1 34.7 us: shards(): pl.pallas_call(spread_kernel, out_shape=(pltpu.VMEM((32, 2, PART, HEAD_DI...]
    pallas_call x1, Pallas kernels: 16.1 us -> 11.7 us  [shards(): pl.pallas_call(merge_kernel, out_shape=jax.ShapeDtypeStruct(queries.shape...]
    unnamed x1 -> x11, local copies, waits for them, and re-layouts: 1.67 us -> 5.05 us
where the time goes in v2:
time: 71.4 us; the launch traced here: 71.1 us
  Pallas kernels  66 us (92%)
  local copies, waits for them, and re-layouts  5.05 us (7%)
    pallas_call x1, Pallas kernels, shards(): pl.pallas_call(spread_kernel, out_shape=(pltpu.VMEM((32, 2, PART, HEAD_DI...  34.7 us
    pallas_call x1, Pallas kernels, shards(): pl.pallas_call(attend_kernel, out_shape=(pltpu.VMEM((8, 2 * GROUP, HEAD_D...  19.7 us
    pallas_call x1, Pallas kernels, shards(): pl.pallas_call(merge_kernel, out_shape=jax.ShapeDtypeStruct(queries.shape...  11.7 us
    unnamed x11, local copies, waits for them, and re-layouts  5.05 us

profile of v2, /device:TPU:8, one launch (start us, length us, event | category | flops | bytes accessed | tf_op | source)
XLA Modules:
  0.0 71.1 jit_solution(11684684316300798499)
XLA Ops:
  0.0 0.0 copy-start
  0.0 0.9 %copy-done = bf16[256,512]{1,0:T(8,128)(2,1)S(1)} copy-done((bf16[256,512]{1,0:T(8,128)(2,1)S(1)}, bf16[256,512]{1,0:T(8,128)(2,1)}, u32[]{:S(2)}) %copy-start) | copy-done | bytes 262168
  1.0 0.0 copy-start.1
  1.0 0.9 %copy-done.1 = bf16[256,512]{1,0:T(8,128)(2,1)S(1)} copy-done((bf16[256,512]{1,0:T(8,128)(2,1)S(1)}, bf16[256,512]{1,0:T(8,128)(2,1)}, u32[]{:S(2)}) %copy-start.1) | copy-done | bytes 262168
  1.9 0.0 copy-start.2
  1.9 0.9 %copy-done.2 = bf16[256,512]{1,0:T(8,128)(2,1)S(1)} copy-done((bf16[256,512]{1,0:T(8,128)(2,1)S(1)}, bf16[256,512]{1,0:T(8,128)(2,1)}, u32[]{:S(2)}) %copy-start.2) | copy-done | bytes 262168
  2.9 0.0 copy-start.3
  2.9 0.8 %copy-done.3 = s32[16384]{0:T(1024)S(1)} copy-done((s32[16384]{0:T(1024)S(1)}, s32[16384]{0:T(1024)}, u32[]{:S(2)}) %copy-start.3) | copy-done | bytes 65560
  3.7 0.0 copy-start.4
  3.7 0.7 copy-done.4
  4.3 34.7 %shard_map.55 = (bf16[32,2,272,128]{3,2,1,0:T(8,128)(2,1)S(1)}, bf16[8,272,128]{2,1,0:T(8,128)(2,1)S(1)}, s32[16,128]{1,0:T(8,128)S(1)}) custom-call(bf16[256,512]{1,0:T(8,128)(2,1)S(1)} %copy-done, bf16[256,512]{1,0:T(8,128)(2,1)S(1)} %copy-done.1, bf16[256,512]{1,0:T(8,128)(2,1)S(1)} %copy-done.2, s32[1,2]{1,0:T(1,128)S(1)} %copy-done.4, ...), custom_call_target="tpu_custom_call" | custom-call | tf_op jit(solution)/shard_map/pallas_call | solution.py:334
  39.0 19.7 %shard_map.56 = (bf16[8,256,128]{2,1,0:T(8,128)(2,1)S(1)}, f32[8,8,128]{2,1,0:T(8,128)S(1)}) custom-call(bf16[32,2,272,128]{3,2,1,0:T(8,128)(2,1)S(1)} %get-tuple-element.10.kv, bf16[8,272,128]{2,1,0:T(8,128)(2,1)S(1)} %get-tuple-element.11.q, s32[16,128]{1,0:T(8,128)S(1)} %get-tuple-element.12.start_ref), custom_call_target="tpu_custom_call" | custom-call | tf_op jit(solution)/shard_map/pallas_call | solution.py:349
  58.7 11.7 %shard_map.57 = bf16[256,512]{1,0:T(8,128)(2,1)S(1)} custom-call(bf16[8,256,128]{2,1,0:T(8,128)(2,1)S(1)} %get-tuple-element.13.o_ref, f32[8,8,128]{2,1,0:T(8,128)S(1)} %get-tuple-element.14.l_ref), custom_call_target="tpu_custom_call" | custom-call | tf_op jit(solution)/shard_map/pallas_call | solution.py:371
  70.4 0.7 copy.7
Async XLA Ops:
  0.0 0.9 %copy-start = (bf16[256,512]{1,0:T(8,128)(2,1)S(1)}, bf16[256,512]{1,0:T(8,128)(2,1)}, u32[]{:S(2)}) copy-start(bf16[256,512]{1,0:T(8,128)(2,1)} %q_ref.1) | copy-start | bytes 786436
  1.0 0.9 %copy-start.1 = (bf16[256,512]{1,0:T(8,128)(2,1)S(1)}, bf16[256,512]{1,0:T(8,128)(2,1)}, u32[]{:S(2)}) copy-start(bf16[256,512]{1,0:T(8,128)(2,1)} %k_ref.1) | copy-start | bytes 786436
  1.9 0.9 %copy-start.2 = (bf16[256,512]{1,0:T(8,128)(2,1)S(1)}, bf16[256,512]{1,0:T(8,128)(2,1)}, u32[]{:S(2)}) copy-start(bf16[256,512]{1,0:T(8,128)(2,1)} %v_ref.1) | copy-start | bytes 786436
  2.9 0.8 %copy-start.3 = (s32[16384]{0:T(1024)S(1)}, s32[16384]{0:T(1024)}, u32[]{:S(2)}) copy-start(s32[16384]{0:T(1024)} %param.9) | copy-start | bytes 196612
  3.7 0.7 copy-start.4
